TPU v7x, 32 devices: a whole 2x2x4 slice. The times are simulated.
32 devices in a mesh: blk: 4 (over y, x), rows: 8 (over z, core).
Axes of the slice: x: 2, y: 2, z: 4, core: 2. Of those that a mesh axis runs over, the one named last changes fastest.
Arguments:
- embeddings: bfloat16 [65536, 768], P(('blk', 'rows')), may hold values from -6 to 6
- coverage: float32 [65536], P(('blk', 'rows')), may hold values from 0 to 4
- chosen_index: int32 [64], replicated, may hold values from 0 to 65535, as said below
- candidate_index: int32 [512], P('blk'), may hold values from 0 to 65535, as said below
Outputs:
- new_coverage: float32 [65536], P(('blk', 'rows'))
- gains: float32 [512], P(('blk', 'rows'))
Inputs may be any that keep to these rules, and one draw needn't show every extreme that they name: `chosen_index`: the entries are distinct; the rows r * 2048 to (r + 1) * 2048 - 1 hold at most 4 of them for every r, and exactly 4 for some r. `candidate_index`: entries b * 128 to (b + 1) * 128 - 1 lie in rows b * 16384 to (b + 1) * 16384 - 1.
All inputs are finite; a program needn't handle non-finite values.
Results may differ from a plain program's by a relative error of at most 0.00035.
Values may be sent and summed in bfloat16 or wider, within the bound.
A program may use at most 64 MiB of HBM per device.

v0:
```python
import jax
import jax.numpy as jnp
from jax import lax
from jax.sharding import PartitionSpec as P


def owned_rows(embeddings, indices, base_row):
    local_rows = embeddings.shape[0]
    offset = indices - base_row
    inside = (offset >= 0) & (offset < local_rows)
    safe = jnp.clip(offset, 0, local_rows - 1)
    picked = jnp.take(embeddings, safe, axis=0).astype(jnp.float32)
    return jnp.where(inside[:, None], picked, 0.0)


def local(embeddings, coverage, chosen_index, candidate_index):
    local_rows = embeddings.shape[0]
    width = embeddings.shape[1]
    scale = 1.0 / width**0.5
    device_pos = lax.axis_index("blk") * lax.axis_size("rows") + lax.axis_index("rows")
    base_row = device_pos * local_rows
    chosen_f = lax.psum(owned_rows(embeddings, chosen_index, base_row), ("blk", "rows"))
    chosen_rows = chosen_f.astype(jnp.bfloat16)
    sims = jnp.dot(embeddings, chosen_rows.T, preferred_element_type=jnp.float32) * scale
    best = jnp.max(sims, axis=1)
    new_coverage = jnp.maximum(coverage, best)
    block_f = lax.psum(
        owned_rows(embeddings, candidate_index, base_row).astype(jnp.bfloat16), "rows"
    )
    cand_sims = (
        jnp.dot(
            embeddings,
            lax.all_gather(block_f, "blk", axis=0, tiled=True).T,
            preferred_element_type=jnp.float32,
        )
        * scale
    )
    gain_part = jnp.sum(jnp.maximum(cand_sims - new_coverage[:, None], 0.0), axis=0)
    gains = lax.psum_scatter(gain_part, ("blk", "rows"), scatter_dimension=0, tiled=True)
    return (new_coverage, gains)


def solution(mesh):
    placed = (P(("blk", "rows"), None), P(("blk", "rows")), P(), P("blk"))
    return jax.shard_map(
        local,
        mesh=mesh,
        in_specs=placed,
        out_specs=(P(("blk", "rows")), P(("blk", "rows"))),
        check_vma=False,
    )
```

profile of v0, /device:TPU:0, one launch (start us, length us, event | category | flops | bytes accessed | tf_op | source)
XLA Modules:
  0.0 129.1 jit_solution(3781930005201907829)
XLA Ops:
  7.2 0.0 copy-start
  7.2 0.0 all-reduce.4.cloned.1.call-start
  7.2 0.8 compare_and_fusion
  8.1 1.0 copy-done
  9.1 0.0 copy-start.1
  9.1 0.9 gather_fusion.1
  9.9 0.8 select_convert_fusion
  10.8 0.0 all-reduce.4.cloned.1.call-update
  10.8 0.7 compare_and_fusion.2
  11.5 0.7 gather_fusion
  12.2 0.1 convert_select_fusion
  12.3 44.4 %all-reduce.5 = bf16[64,768]{1,0:T(8,128)(2,1)S(1)} all-reduce(f32[64,768]{1,0:T(8,128)S(1)} %convert_select_fusion), channel_id=1, replica_groups=mesh['blk'=4,'rows'=8] {'blk','rows'}, use_global_device_ids=true, to_apply=%region_0.1 | all-reduce | flops 49152 | bytes 294912 | tf_op jit(solution)/shard_map/psum | solution.py:22
  56.7 1.1 fusion
  57.8 0.0 copy-done.1
  57.8 0.0 copy-start.2
  57.8 11.1 %all-reduce.4.cloned.1.call-done = bf16[128,768]{1,0:T(8,128)(2,1)} async-done(((bf16[128,768]{1,0:T(8,128)(2,1)}), bf16[128,768]{1,0:T(8,128)(2,1)}) %all-reduce.4.cloned.1.call-update) | async-done | bytes 196624 | tf_op jit(solution)/shard_map/psum | solution.py:27
  68.9 12.4 %all_gather.3 = bf16[512,768]{1,0:T(8,128)(2,1)S(1)} all-gather(bf16[128,768]{1,0:T(8,128)(2,1)} %all-reduce.4.cloned.1.call-done), channel_id=1, replica_groups=mesh['blk'=4,'rows'=8] {'blk'}, dimensions={0}, use_global_device_ids=true | all-gather | bytes 983040 | tf_op jit(solution)/shard_map/all_gather | solution.py:33
  81.3 1.9 %maximum_reduce_fusion = f32[512]{0:T(512)S(1)} fusion(bf16[512,768]{1,0:T(8,128)(2,1)S(1)} %all_gather.3, bf16[2048,768]{1,0:T(8,128)(2,1)S(1)} %copy-done, f32[2048]{0:T(1024)S(1)} %max.18), kind=kOutput, calls=%fused_computation.2 | convolution fusion | flops 1614806528 | bytes 3942400 | tf_op jit(solution)/shard_map/dot_general | solution.py:31
  83.3 0.0 copy-done.2
  83.3 38.4 %all-reduce = f32[512]{0:T(512)S(1)} all-reduce(f32[512]{0:T(512)S(1)} %maximum_reduce_fusion), channel_id=2, replica_groups=mesh['blk'=4,'rows'=8] {'blk','rows'}, use_global_device_ids=true, to_apply=%region_4.5.clone | all-reduce | flops 512 | bytes 4096
  121.6 0.6 dynamic-slice
  (3 shorter events, 0.0 us)
Async XLA Ops:
  7.2 1.9 %copy-start = (bf16[2048,768]{1,0:T(8,128)(2,1)S(1)}, bf16[2048,768]{1,0:T(8,128)(2,1)}, u32[]{:S(2)}) copy-start(bf16[2048,768]{1,0:T(8,128)(2,1)} %param.4) | copy-start | bytes 9437188
  7.2 61.7 %all-reduce.4.cloned.1.call-start = ((), (), s32[]{:S(2)}) async-start(), calls=%async_computation | async-start | bytes 393216 | tf_op jit(solution)/shard_map/psum | solution.py:27
  9.1 48.7 %copy-start.1 = (f32[2048]{0:T(1024)S(1)}, f32[2048]{0:T(1024)}, u32[]{:S(2)}) copy-start(f32[2048]{0:T(1024)} %param.5) | copy-start | bytes 24580
  57.8 25.5 %copy-start.2 = (f32[2048]{0:T(1024)}, f32[2048]{0:T(1024)S(1)}, u32[]{:S(2)}) copy-start(f32[2048]{0:T(1024)S(1)} %max.18) | copy-start | bytes 24580
Sparse Core Ops, SparseCore 0:
  10.9 57.9 all-reduce.3
where the time goes:
time: 129 us
  blocking collectives  95.2 us (74%)
  between operations  14.1 us (11%)
  waiting for transfers between devices  11.1 us (9%)
  local copies, waits for them, and re-layouts  3.2 us (2%)
  matrix products  3 us (2%)
  other arithmetic  2.41 us (2%)
    psum x1, blocking collectives, local(): lax.psum(owned_rows(embeddings, chosen_index, base_row), ('blk', 'rows'))  44.4 us
    unnamed x1, blocking collectives  38.4 us
    all_gather x1, blocking collectives, local(): lax.all_gather(block_f, 'blk', axis=0, tiled=True)  12.4 us
    psum x1, waiting for transfers between devices, local(): lax.psum(owned_rows(embeddings, candidate_index, base_row).astype(jnp.bfl...  11.1 us
  transfers between devices with their start and end apart: 1, of which 1 were waited for; matrix products, arithmetic and copies ran while one was open for 2% of the time, Pallas kernels for 0%

commit v1 on v0

--- a/solution.py
+++ b/solution.py
@@ -19,7 +19,9 @@
     scale = 1.0 / width**0.5
     device_pos = lax.axis_index("blk") * lax.axis_size("rows") + lax.axis_index("rows")
     base_row = device_pos * local_rows
-    chosen_f = lax.psum(owned_rows(embeddings, chosen_index, base_row), ("blk", "rows"))
+    chosen_f = lax.psum(
+        lax.psum(owned_rows(embeddings, chosen_index, base_row), axis_name="rows"), axis_name="blk"
+    )
     chosen_rows = chosen_f.astype(jnp.bfloat16)
     sims = jnp.dot(embeddings, chosen_rows.T, preferred_element_type=jnp.float32) * scale
     best = jnp.max(sims, axis=1)

time: 129 us -> 186 us (1.44)
  waiting for transfers between devices: 11.1 us -> 91.5 us
  blocking collectives: 95.2 us -> 70.5 us
    psum x0 -> x1, waiting for transfers between devices: none -> 55.7 us  [local(): lax.psum(owned_rows(embeddings, chosen_index, base_row), axis_name='rows')]
    psum x1, waiting for transfers between devices: 11.1 us -> 35.9 us  [local(): lax.psum(owned_rows(embeddings, candidate_index, base_row).astype(jnp.bfl...]
    psum x1, blocking collectives: 44.4 us -> 19.6 us  [local(): lax.psum(lax.psum(owned_rows(embeddings, chosen_index, base_row), axis_na...]
  transfers between devices with their start and end apart: 1 -> 2, of which waited for: 1 -> 2; matrix products, arithmetic and copies ran while one was open for 2% -> 2% of each run, Pallas kernels for 0% -> 0%
where the time goes in v1:
time: 186 us; the launch traced here: 185 us
  waiting for transfers between devices  91.5 us (49%)
  blocking collectives  70.5 us (38%)
  between operations  14.1 us (8%)
  local copies, waits for them, and re-layouts  3.2 us (2%)
  other arithmetic  3.08 us (2%)
  matrix products  3 us (2%)
    psum x1, waiting for transfers between devices, local(): lax.psum(owned_rows(embeddings, chosen_index, base_row), axis_name='rows')  55.7 us
    unnamed x1, blocking collectives  38.4 us
    psum x1, waiting for transfers between devices, local(): lax.psum(owned_rows(embeddings, candidate_index, base_row).astype(jnp.bfl...  35.9 us
    psum x1, blocking collectives, local(): lax.psum(lax.psum(owned_rows(embeddings, chosen_index, base_row), axis_na...  19.6 us
    all_gather x1, blocking collectives, local(): lax.all_gather(block_f, 'blk', axis=0, tiled=True)  12.4 us
  transfers between devices with their start and end apart: 2, of which 2 were waited for; matrix products, arithmetic and copies ran while one was open for 2% of the time, Pallas kernels for 0%

profile of v1, /device:TPU:0, one launch (start us, length us, event | category | flops | bytes accessed | tf_op | source)
XLA Modules:
  0.0 185.5 jit_solution(1596013340467307572)
XLA Ops:
  7.2 0.0 copy-start
  7.2 0.0 all-reduce.5.cloned.1.call-start
  7.2 0.8 compare_and_fusion.2
  8.1 1.0 copy-done
  9.1 0.7 gather_fusion
  9.8 0.8 convert_select_fusion
  10.5 0.0 copy-start.1
  10.5 0.0 all-reduce.5.cloned.1.call-update
  10.6 0.0 all-reduce.7.cloned.1.call-start
  10.6 0.7 compare_and_fusion
  11.3 0.9 gather_fusion.1
  12.2 0.8 select_convert_fusion
  13.0 0.0 all-reduce.7.cloned.1.call-update
  13.0 55.7 %all-reduce.5.cloned.1.call-done = f32[64,768]{1,0:T(8,128)} async-done(((f32[64,768]{1,0:T(8,128)}), f32[64,768]{1,0:T(8,128)}) %all-reduce.5.cloned.1.call-update) | async-done | bytes 196624 | tf_op jit(solution)/shard_map/psum | solution.py:23
  68.7 19.6 %all-reduce.8 = bf16[64,768]{1,0:T(8,128)(2,1)S(1)} all-reduce(f32[64,768]{1,0:T(8,128)} %all-reduce.5.cloned.1.call-done), channel_id=1, replica_groups=mesh['blk'=4,'rows'=8] {'blk'}, use_global_device_ids=true, to_apply=%region_1.2 | all-reduce | flops 49152 | bytes 294912 | tf_op jit(solution)/shard_map/psum | solution.py:22
  88.3 1.1 fusion
  89.4 0.0 copy-done.1
  89.4 0.0 copy-start.2
  89.4 35.9 %all-reduce.7.cloned.1.call-done = bf16[128,768]{1,0:T(8,128)(2,1)} async-done(((bf16[128,768]{1,0:T(8,128)(2,1)}), bf16[128,768]{1,0:T(8,128)(2,1)}) %all-reduce.7.cloned.1.call-update) | async-done | bytes 196624 | tf_op jit(solution)/shard_map/psum | solution.py:29
  125.3 12.4 %all_gather.3 = bf16[512,768]{1,0:T(8,128)(2,1)S(1)} all-gather(bf16[128,768]{1,0:T(8,128)(2,1)} %all-reduce.7.cloned.1.call-done), channel_id=1, replica_groups=mesh['blk'=4,'rows'=8] {'blk'}, dimensions={0}, use_global_device_ids=true | all-gather | bytes 983040 | tf_op jit(solution)/shard_map/all_gather | solution.py:35
  137.7 1.9 %maximum_reduce_fusion = f32[512]{0:T(512)S(1)} fusion(bf16[512,768]{1,0:T(8,128)(2,1)S(1)} %all_gather.3, bf16[2048,768]{1,0:T(8,128)(2,1)S(1)} %copy-done, f32[2048]{0:T(1024)S(1)} %max.18), kind=kOutput, calls=%fused_computation.2 | convolution fusion | flops 1614806528 | bytes 3942400 | tf_op jit(solution)/shard_map/dot_general | solution.py:33
  139.7 0.0 copy-done.2
  139.7 38.4 %all-reduce = f32[512]{0:T(512)S(1)} all-reduce(f32[512]{0:T(512)S(1)} %maximum_reduce_fusion), channel_id=2, replica_groups=mesh['blk'=4,'rows'=8] {'blk','rows'}, use_global_device_ids=true, to_apply=%region_5.6.clone | all-reduce | flops 512 | bytes 4096
  178.0 0.6 dynamic-slice
  (3 shorter events, 0.0 us)
Async XLA Ops:
  7.2 1.9 %copy-start = (bf16[2048,768]{1,0:T(8,128)(2,1)S(1)}, bf16[2048,768]{1,0:T(8,128)(2,1)}, u32[]{:S(2)}) copy-start(bf16[2048,768]{1,0:T(8,128)(2,1)} %param.4) | copy-start | bytes 9437188
  7.2 61.5 %all-reduce.5.cloned.1.call-start = ((), (), s32[]{:S(2)}) async-start(), calls=%async_computation | async-start | bytes 393216 | tf_op jit(solution)/shard_map/psum | solution.py:23
  10.5 78.9 %copy-start.1 = (f32[2048]{0:T(1024)S(1)}, f32[2048]{0:T(1024)}, u32[]{:S(2)}) copy-start(f32[2048]{0:T(1024)} %param.5) | copy-start | bytes 24580
  10.6 114.7 %all-reduce.7.cloned.1.call-start = ((), (), s32[]{:S(2)}) async-start(), calls=%async_computation.1 | async-start | bytes 393216 | tf_op jit(solution)/shard_map/psum | solution.py:29
  89.4 50.2 %copy-start.2 = (f32[2048]{0:T(1024)}, f32[2048]{0:T(1024)S(1)}, u32[]{:S(2)}) copy-start(f32[2048]{0:T(1024)S(1)} %max.18) | copy-start | bytes 24580
Sparse Core Ops, SparseCore 0:
  10.7 57.9 all-reduce.4
  71.0 54.2 all-reduce.6
